TPU v7x, 32 devices: a whole 2x2x4 slice. The times are simulated.
32 devices in a mesh: outer: 4 (over y, core), inner: 8 (over z, x).
Axes of the slice: x: 2, y: 2, z: 4, core: 2. Of those that a mesh axis runs over, the one named last changes fastest.
Arguments:
- amplitudes: float32 [2, 8388608], P(None, ('outer', 'inner')), may hold values from -200 to 200
Outputs:
- transformed: float32 [2, 8388608], P(None, ('outer', 'inner'))
- checks: float32 [3], replicated
All inputs are finite; a program needn't handle non-finite values.
Results may differ from a plain program's by a relative error of at most 0.00007.
Values sent between devices are 32-bit elements; how exact they have to be, the bound alone decides.
A program may use at most 64 MiB of HBM per device.

v0:
```python
import functools
import math

import jax
import jax.numpy as jnp
import numpy as np
from jax import lax
from jax.experimental import pallas as pl
from jax.experimental.pallas import tpu as pltpu
from jax.sharding import PartitionSpec as P

WINDOW = 9
COLUMNS = 2**WINDOW
LANES = 128
SUB = 8
RADIX = COLUMNS // LANES
MESH = pl.DeviceIdType.MESH


def rev(value, count):
    out = 0
    for bit in range(count):
        out |= (value >> bit & 1) << (count - 1 - bit)
    return out


def split_bf16(values):
    high = values.astype(jnp.bfloat16)
    return high, (values - high.astype(np.float32)).astype(jnp.bfloat16)


def tables(rows_count, n_devices):
    f = np.arange(COLUMNS).reshape(LANES, RADIX).T
    lane = np.arange(LANES)
    ang = (f[:, :, None] * lane) % COLUMNS * (2.0 * np.pi / COLUMNS)
    c, s = np.cos(ang) / math.sqrt(COLUMNS), np.sin(ang) / math.sqrt(COLUMNS)
    table = np.stack([np.concatenate([c, -s], -1), np.concatenate([s, c], -1)], 2)
    table = table.reshape(RADIX, 2 * LANES, 2 * LANES).astype(np.float32)
    fa = f * (2.0 * np.pi / COLUMNS)
    cf = np.zeros((RADIX, SUB, LANES, 2), np.float32)
    cf[:, 0, :, 0], cf[:, 0, :, 1] = np.cos(fa), np.sin(fa)
    cf[:, 1, :, 0], cf[:, 1, :, 1] = -np.sin(fa), np.cos(fa)
    cf = cf.reshape(RADIX, SUB, 2 * LANES)
    bits = rows_count.bit_length() - 1
    ra = np.array([rev(r, bits) for r in range(rows_count)]) * (2.0 * np.pi / (rows_count * COLUMNS))
    cr = np.zeros((SUB, rows_count), np.float32)
    cr[0], cr[1] = np.cos(ra), np.sin(ra)
    return table, cf, cr


def swap_sublanes(v):
    at = lax.broadcasted_iota(jnp.int32, v.shape, 1)
    up, down = pltpu.roll(v, 5, 1), pltpu.roll(v, 3, 1)
    v = jnp.where((at == 1) | (at == 3), up, v)
    return jnp.where((at == 4) | (at == 6), down, v)


def kernel(n_outer, n_inner, rows_count, total_len, x_ref, th_ref, tl_ref, cf_ref, cr_ref, out_ref, tot_ref,
           sendbuf, recv, stat_out, stats, send_sem, recv_sem, own_sem, ssend_sem, srecv_sem):
    n_devices = n_outer * n_inner
    obits, ibits = n_outer.bit_length() - 1, n_inner.bit_length() - 1
    o, i = lax.axis_index("outer"), lax.axis_index("inner")
    me = o * n_inner + i
    slot = 0
    odelta, idelta = [], []
    for k in range(obits):
        bit = o // 2**k % 2
        slot = slot + bit * 2 ** (obits - 1 - k)
        odelta.append((1 - 2 * bit) * 2**k)
    for k in range(ibits):
        bit = i // 2**k % 2
        slot = slot + bit * 2 ** (ibits - 1 - k) * n_outer
        idelta.append((1 - 2 * bit) * 2**k)

    def peer(mo, mi):
        po, pi = o, i
        for k in range(obits):
            if mo >> k & 1:
                po = po + odelta[k]
        for k in range(ibits):
            if mi >> k & 1:
                pi = pi + idelta[k]
        return po, pi

    masks = [(mo, mi) for mi in reversed(range(n_inner)) for mo in reversed(range(n_outer)) if mo or mi]
    peers = [peer(mo, mi) for mo, mi in masks]

    barrier = pltpu.get_barrier_semaphore()
    for p in peers:
        pl.semaphore_signal(barrier, inc=1, device_id=p, device_id_type=MESH)

    groups = rows_count // LANES
    block = SUB * groups

    def data_copy(chunk, n):
        po, pi = peers[n]
        e = po * n_inner + pi
        return pltpu.make_async_remote_copy(
            src_ref=sendbuf.at[pl.ds(pl.multiple_of((chunk * n_devices + e) * block, block), block)],
            dst_ref=recv.at[pl.ds(pl.multiple_of((chunk * n_devices + slot) * block, block), block)],
            send_sem=send_sem.at[chunk, n], recv_sem=recv_sem.at[chunk, n],
            device_id=peers[n], device_id_type=MESH)

    def own_copy(chunk):
        return pltpu.make_async_copy(
            sendbuf.at[pl.ds(pl.multiple_of((chunk * n_devices + me) * block, block), block)],
            recv.at[pl.ds(pl.multiple_of((chunk * n_devices + slot) * block, block), block)],
            own_sem.at[chunk])

    def stat_copy(n):
        return pltpu.make_async_remote_copy(
            src_ref=stat_out, dst_ref=stats.at[slot],
            send_sem=ssend_sem.at[n], recv_sem=srecv_sem.at[n],
            device_id=peers[n], device_id_type=MESH)

    dims = (((1,), (1,)), ((), ()))
    parts = [[x_ref[pl.ds(2 * ct + s, rows_count, stride=2 * RADIX), :] for s in range(2)] for ct in range(RADIX)]
    (x0r, x0i), (x1r, x1i), (x2r, x2i), (x3r, x3i) = parts
    ar, ai, br, bi = x0r + x2r, x0i + x2i, x0r - x2r, x0i - x2i
    cr_, ci_, dr, di = x1r + x3r, x1i + x3i, x1r - x3r, x1i - x3i
    mixed = [(ar + cr_, ai + ci_), (br - di, bi + dr), (ar - cr_, ai - ci_), (br + di, bi - dr)]
    squares = jnp.zeros((SUB, LANES), jnp.float32)
    z = jnp.zeros((SUB, rows_count), jnp.float32)
    for chunk in range(RADIX):
        b = jnp.concatenate(mixed[chunk], 1)
        bh, bl = split_bf16(b)
        th, tl = th_ref[chunk], tl_ref[chunk]
        res = lax.dot_general(th, bh, dims, preferred_element_type=jnp.float32)
        res += lax.dot_general(th, bl, dims, preferred_element_type=jnp.float32)
        res += lax.dot_general(tl, bh, dims, preferred_element_type=jnp.float32)
        for e in range(n_devices):
            for g in range(groups):
                sendbuf[pl.ds(((chunk * n_devices + e) * groups + g) * SUB, SUB), :] = (
                    res[e * SUB:(e + 1) * SUB, g * LANES:(g + 1) * LANES])
        z += jnp.dot(cf_ref[chunk], res, precision=lax.Precision.HIGHEST, preferred_element_type=jnp.float32)
        sq = jnp.sum((res * res).reshape(-1, SUB, rows_count), 0)
        for g in range(groups):
            squares += sq[:, g * LANES:(g + 1) * LANES]
        if chunk == 0:
            pl.semaphore_wait(barrier, len(peers))
        if chunk == RADIX - 1:
            cosr, sinr, zr, zi = cr_ref[0:1, :], cr_ref[1:2, :], z[0:1, :], z[1:2, :]
            zre, zim = zr * cosr + zi * sinr, zi * cosr - zr * sinr
            fold = lambda v: sum(v[:, g * LANES:(g + 1) * LANES] for g in range(groups))
            stat_out[...] = jnp.concatenate(
                [jnp.sum(squares, 0, keepdims=True), fold(zre), fold(zim),
                 jnp.zeros((SUB - 3, LANES), jnp.float32)], 0)
            stats[pl.ds(slot, 1)] = stat_out[...][None]
            for n in range(len(peers)):
                stat_copy(n).start()
        for n in range(len(peers)):
            data_copy(chunk, n).start()
        own_copy(chunk).start()

    gbits = groups.bit_length() - 1
    for chunk in range(RADIX):
        for n in range(len(peers)):
            data_copy(chunk, n).wait_recv()
        own_copy(chunk).wait()
        for h in range(SUB):
            g = (h // 2) * RADIX + chunk
            tile = jnp.concatenate(
                [recv[pl.ds((chunk * n_devices * groups + rev(j, gbits)) * SUB + h, n_devices, stride=block), :]
                 for j in range(groups)], 0)
            turned = swap_sublanes(tile.T.reshape(LANES // SUB, SUB, LANES))
            for a in range(LANES // SUB):
                out_ref[pl.ds((g * LANES + rev(a, 4)) * 2 + h % 2, SUB, stride=2 * LANES // SUB), :] = turned[a]

    for n in range(len(peers)):
        stat_copy(n).wait_recv()
    t0 = t1 = t2 = jnp.zeros((SUB, LANES), jnp.float32)
    for q in range(n_devices):
        angle = 2.0 * math.pi * q / total_len
        v = stats[q]
        t0, t1, t2 = t0 + v, t1 + v * math.cos(angle), t2 + v * math.sin(angle)
    re = t1[1:2] + t2[2:3]
    im = t1[2:3] - t2[1:2]
    sums = jnp.concatenate([t0[0:1], re, im, jnp.zeros((SUB - 3, LANES), jnp.float32)], 0)
    tot_ref[...] = jnp.broadcast_to(jnp.sum(sums, 1, keepdims=True), (SUB, LANES))
    for n in range(len(peers)):
        stat_copy(n).wait_send()
        for chunk in range(RADIX):
            data_copy(chunk, n).wait_send()


def fast(n_outer, n_inner, amplitudes):
    amp_dev = amplitudes.shape[1]
    n_devices = n_outer * n_inner
    rows_count = amp_dev // COLUMNS
    total_len = amp_dev * n_devices
    view = amplitudes.reshape(2, amp_dev // LANES, LANES).transpose(1, 0, 2).reshape(-1, LANES)
    table, cf, cr = tables(rows_count, n_devices)
    th = table.astype(jnp.bfloat16)
    tl = (table - th.astype(np.float32)).astype(jnp.bfloat16)
    vmem = pl.BlockSpec(memory_space=pltpu.VMEM)
    n_peers = n_devices - 1
    field, tot = pl.pallas_call(
        functools.partial(kernel, n_outer, n_inner, rows_count, total_len),
        out_shape=(jax.ShapeDtypeStruct(view.shape, jnp.float32), jax.ShapeDtypeStruct((SUB, LANES), jnp.float32)),
        in_specs=[vmem] * 5,
        out_specs=(vmem, vmem),
        scratch_shapes=[
            pltpu.VMEM(view.shape, jnp.float32),
            pltpu.VMEM(view.shape, jnp.float32),
            pltpu.VMEM((SUB, LANES), jnp.float32),
            pltpu.VMEM((n_devices, SUB, LANES), jnp.float32),
            pltpu.SemaphoreType.DMA((RADIX, n_peers)),
            pltpu.SemaphoreType.DMA((RADIX, n_peers)),
            pltpu.SemaphoreType.DMA((RADIX,)),
            pltpu.SemaphoreType.DMA((n_peers,)),
            pltpu.SemaphoreType.DMA((n_peers,)),
        ],
        compiler_params=pltpu.CompilerParams(collective_id=0, has_side_effects=True,
                                             vmem_limit_bytes=32 * 2**20),
    )(view, jnp.asarray(th), jnp.asarray(tl), jnp.asarray(cf), jnp.asarray(cr))
    mean_square = tot[0, 0] / total_len
    factor = lax.rsqrt(mean_square + 1e-06)
    scaled = factor / math.sqrt(total_len)
    checks = jnp.stack([mean_square, tot[1, 0] * scaled, tot[2, 0] * scaled])
    result = (field * factor).reshape(-1, 2, LANES).transpose(1, 0, 2).reshape(2, amp_dev)
    return result, checks


def reverse_index(values, count):
    result = jnp.zeros_like(values)
    for bit_pos in range(count):
        result = result | (values >> bit_pos & 1) << count - 1 - bit_pos
    return result


def reversal_table(size, count):
    indices = jnp.arange(size, dtype=jnp.int32)
    return (reverse_index(indices, count)[:, None] == indices[None, :]).astype(jnp.float32)


def check_terms(current, positions, angle_scale):
    angles = positions.astype(jnp.float32) * angle_scale
    cosine = jnp.cos(angles)
    sine = jnp.sin(angles)
    squares = jnp.sum(current * current)
    phase_real = jnp.sum(current[0] * cosine + current[1] * sine)
    phase_imag = jnp.sum(current[1] * cosine - current[0] * sine)
    return (squares, phase_real, phase_imag)


def per_device(amplitudes):
    amp_dev = amplitudes.shape[1]
    n_outer = lax.axis_size("outer")
    n_inner = lax.axis_size("inner")
    outer_bits = n_outer.bit_length() - 1
    inner_bits = n_inner.bit_length() - 1
    global_bits = outer_bits + inner_bits
    local_bits = amp_dev.bit_length() - 1
    n_devices = n_outer * n_inner
    high_count = amp_dev // n_devices
    total_len = amp_dev * n_devices
    columns = 2**WINDOW
    rows_count = amp_dev // columns
    column_ids = jnp.arange(columns, dtype=jnp.int32)
    reversed_ids = reverse_index(column_ids, WINDOW)
    products = column_ids[:, None] * reversed_ids[None, :] % columns
    angles = products.astype(jnp.float32) * (2.0 * math.pi / columns)
    real_part = jnp.cos(angles) / math.sqrt(columns)
    imag_part = jnp.sin(angles) / math.sqrt(columns)
    table = jnp.concatenate(
        [jnp.concatenate([real_part, imag_part], 1), jnp.concatenate([-imag_part, real_part], 1)], 0
    )
    stacked = jnp.concatenate(
        [amplitudes[0].reshape(rows_count, columns), amplitudes[1].reshape(rows_count, columns)], 1
    )
    result = jnp.dot(
        stacked, table, precision=lax.Precision.HIGHEST, preferred_element_type=jnp.float32
    )
    windowed = jnp.stack([result[:, :columns].reshape(-1), result[:, columns:].reshape(-1)])
    device_id = lax.axis_index("outer") * n_inner + lax.axis_index("inner")
    angle_scale = 2.0 * math.pi / total_len
    local_ids = jnp.arange(amp_dev, dtype=jnp.int32)
    positions = reverse_index(device_id * amp_dev + local_ids, local_bits + global_bits)
    totals = lax.psum(check_terms(windowed, positions, angle_scale), ("outer", "inner"))
    device_table = reversal_table(n_devices, global_bits)
    high_table = reversal_table(high_count, local_bits - global_bits)
    grid = windowed.reshape(2, high_count, n_devices)
    ordered = jnp.einsum("pm,shm->sph", device_table, grid, precision=lax.Precision.HIGHEST)
    blocks = ordered.reshape(2, n_outer, n_inner, high_count)
    blocks = lax.all_to_all(
        lax.all_to_all(blocks, "outer", split_axis=1, concat_axis=1, tiled=True),
        "inner",
        split_axis=2,
        concat_axis=2,
        tiled=True,
    )
    received = blocks.reshape(2, n_devices, high_count)
    turned_high = jnp.einsum("qh,sdh->sdq", high_table, received, precision=lax.Precision.HIGHEST)
    placed = jnp.einsum("ed,sdq->sqe", device_table, turned_high, precision=lax.Precision.HIGHEST)
    reversed_field = placed.reshape(2, amp_dev)
    mean_square = totals[0] / total_len
    factor = lax.rsqrt(mean_square + 1e-06)
    scaled = factor / math.sqrt(total_len)
    checks = jnp.stack([mean_square, totals[1] * scaled, totals[2] * scaled])
    return (reversed_field * factor, checks)


def solution(mesh):
    n_outer, n_inner = mesh.shape["outer"], mesh.shape["inner"]

    def body(amplitudes):
        rows_count = amplitudes.shape[1] // COLUMNS
        n_devices = n_outer * n_inner
        if rows_count * n_devices == LANES * LANES and n_devices * SUB == 2 * LANES:
            return fast(n_outer, n_inner, amplitudes)
        return per_device(amplitudes)

    return jax.shard_map(
        body,
        mesh=mesh,
        in_specs=(P(None, ("outer", "inner")),),
        out_specs=(P(None, ("outer", "inner")), P()),
        check_vma=False,
    )
```

profile of v0, /device:TPU:0, one launch (start us, length us, event | category | flops | bytes accessed | tf_op | source)
XLA Modules:
  0.0 70.4 jit_solution(6404318154234497395)
XLA Ops:
  0.6 0.0 copy-start
  0.6 1.6 %copy-done = f32[2,262144]{1,0:T(2,128)S(1)} copy-done((f32[2,262144]{1,0:T(2,128)S(1)}, f32[2,262144]{1,0:T(2,128)}, u32[]{:S(2)}) %copy-start) | copy-done | bytes 2097176
  2.2 0.0 copy-start.1
  2.2 1.0 %copy-done.1 = bf16[4,256,256]{2,1,0:T(8,128)(2,1)S(1)} copy-done((bf16[4,256,256]{2,1,0:T(8,128)(2,1)S(1)}, bf16[4,256,256]{2,1,0:T(8,128)(2,1)}, u32[]{:S(2)}) %copy-start.1) | copy-done | bytes 524312
  3.3 0.0 copy-start.2
  3.3 1.0 %copy-done.2 = bf16[4,256,256]{2,1,0:T(8,128)(2,1)S(1)} copy-done((bf16[4,256,256]{2,1,0:T(8,128)(2,1)S(1)}, bf16[4,256,256]{2,1,0:T(8,128)(2,1)}, u32[]{:S(2)}) %copy-start.2) | copy-done | bytes 524312
  4.3 0.0 copy-start.3
  4.3 0.8 %copy-done.3 = f32[4,8,256]{2,1,0:T(8,128)S(1)} copy-done((f32[4,8,256]{2,1,0:T(8,128)S(1)}, f32[4,8,256]{2,1,0:T(8,128)}, u32[]{:S(2)}) %copy-start.3) | copy-done | bytes 32792
  5.1 0.0 copy-start.4
  5.1 0.7 %copy-done.4 = f32[8,512]{1,0:T(8,128)S(1)} copy-done((f32[8,512]{1,0:T(8,128)S(1)}, f32[8,512]{1,0:T(8,128)}, u32[]{:S(2)}) %copy-start.4) | copy-done | bytes 16408
  5.8 60.1 %shard_map.68 = (f32[4096,128]{1,0:T(8,128)S(1)}, f32[8,128]{1,0:T(8,128)S(1)}) custom-call(f32[4096,128]{1,0:T(8,128)S(1)} %bitcast.16, bf16[4,256,256]{2,1,0:T(8,128)(2,1)S(1)} %copy-done.2, bf16[4,256,256]{2,1,0:T(8,128)(2,1)S(1)} %copy-done.1, f32[4,8,256]{2,1,0:T(8,128)S(1)} %copy-done.3, f32[8,512]{1,0:T(8,128)S(1)} %copy-done.4), custom_call_target="tpu_custom_call" | custom-call | tf_op jit(solution)/shard_map/pallas_call | solution.py:197
  65.9 0.5 fusion
  68.4 0.6 pad_maximum_fusion
  68.9 1.5 %broadcast_multiply_fusion = f32[4096,128]{1,0:T(8,128)} fusion(f32[4096,128]{1,0:T(8,128)S(1)} %get-tuple-element.4, f32[]{:T(128)} %bitcast.3), kind=kLoop, calls=%fused_computation | loop fusion | flops 524288 | bytes 4194308 | tf_op jit(solution)/shard_map/mul | solution.py:220
Async XLA Ops:
  0.6 1.6 %copy-start = (f32[2,262144]{1,0:T(2,128)S(1)}, f32[2,262144]{1,0:T(2,128)}, u32[]{:S(2)}) copy-start(f32[2,262144]{1,0:T(2,128)} %param.5) | copy-start | bytes 6291460
  2.2 1.0 %copy-start.1 = (bf16[4,256,256]{2,1,0:T(8,128)(2,1)S(1)}, bf16[4,256,256]{2,1,0:T(8,128)(2,1)}, u32[]{:S(2)}) copy-start(bf16[4,256,256]{2,1,0:T(8,128)(2,1)} %constant.19.clone.tl_ref) | copy-start | bytes 1572868
  3.3 1.0 %copy-start.2 = (bf16[4,256,256]{2,1,0:T(8,128)(2,1)S(1)}, bf16[4,256,256]{2,1,0:T(8,128)(2,1)}, u32[]{:S(2)}) copy-start(bf16[4,256,256]{2,1,0:T(8,128)(2,1)} %constant.18.clone.th_ref) | copy-start | bytes 1572868
  4.3 0.8 %copy-start.3 = (f32[4,8,256]{2,1,0:T(8,128)S(1)}, f32[4,8,256]{2,1,0:T(8,128)}, u32[]{:S(2)}) copy-start(f32[4,8,256]{2,1,0:T(8,128)} %constant.20.clone.cf_ref) | copy-start | bytes 98308
  5.1 0.7 %copy-start.4 = (f32[8,512]{1,0:T(8,128)S(1)}, f32[8,512]{1,0:T(8,128)}, u32[]{:S(2)}) copy-start(f32[8,512]{1,0:T(8,128)} %constant.21.clone.cr_ref) | copy-start | bytes 49156
where the time goes:
time: 70.8 us; the launch traced here: 70.4 us
  Pallas kernels  60.1 us (85%)
  local copies, waits for them, and re-layouts  5.66 us (8%)
  between operations  2.55 us (4%)
  other arithmetic  2.04 us (3%)
    pallas_call x1, Pallas kernels, fast(): pl.pallas_call(functools.partial(kernel, n_outer, n_inner, rows_count, to...  60.1 us
    unnamed x10, local copies, waits for them, and re-layouts  5.14 us
    mul x1, other arithmetic, fast(): field * factor  1.45 us

commit v1 on v0

--- a/solution.py
+++ b/solution.py
@@ -55,8 +55,8 @@
     return jnp.where((at == 4) | (at == 6), down, v)
 
 
-def kernel(n_outer, n_inner, rows_count, total_len, x_ref, th_ref, tl_ref, cf_ref, cr_ref, out_ref, tot_ref,
-           sendbuf, recv, stat_out, stats, send_sem, recv_sem, own_sem, ssend_sem, srecv_sem):
+def kernel(n_outer, n_inner, rows_count, total_len, x_hbm, th_hbm, tl_hbm, cf_hbm, cr_hbm, out_hbm, tot_ref, fac_ref,
+           x_ref, th_ref, tl_ref, cf_ref, cr_ref, out_ref, sendbuf, recv, stat_out, stats, send_sem, recv_sem, own_sem, ssend_sem, srecv_sem, load_sem, out_sem):
     n_devices = n_outer * n_inner
     obits, ibits = n_outer.bit_length() - 1, n_inner.bit_length() - 1
     o, i = lax.axis_index("outer"), lax.axis_index("inner")
@@ -82,12 +82,17 @@
                 pi = pi + idelta[k]
         return po, pi
 
-    masks = [(mo, mi) for mi in reversed(range(n_inner)) for mo in reversed(range(n_outer)) if mo or mi]
+    masks = [(mo, mi) for mi in range(n_inner) for mo in range(n_outer) if mo or mi]
     peers = [peer(mo, mi) for mo, mi in masks]
 
     barrier = pltpu.get_barrier_semaphore()
     for p in peers:
         pl.semaphore_signal(barrier, inc=1, device_id=p, device_id_type=MESH)
+
+    loads = [pltpu.make_async_copy(src, dst, load_sem.at[k]) for k, (src, dst) in enumerate(
+        [(x_hbm, x_ref), (th_hbm, th_ref), (tl_hbm, tl_ref), (cf_hbm, cf_ref), (cr_hbm, cr_ref)])]
+    for load in loads:
+        load.start()
 
     groups = rows_count // LANES
     block = SUB * groups
@@ -113,7 +118,13 @@
             send_sem=ssend_sem.at[n], recv_sem=srecv_sem.at[n],
             device_id=peers[n], device_id_type=MESH)
 
+    def send(chunk):
+        for n in range(len(peers)):
+            data_copy(chunk, n).start()
+        own_copy(chunk).start()
+
     dims = (((1,), (1,)), ((), ()))
+    loads[0].wait()
     parts = [[x_ref[pl.ds(2 * ct + s, rows_count, stride=2 * RADIX), :] for s in range(2)] for ct in range(RADIX)]
     (x0r, x0i), (x1r, x1i), (x2r, x2i), (x3r, x3i) = parts
     ar, ai, br, bi = x0r + x2r, x0i + x2i, x0r - x2r, x0i - x2i
@@ -124,6 +135,9 @@
     for chunk in range(RADIX):
         b = jnp.concatenate(mixed[chunk], 1)
         bh, bl = split_bf16(b)
+        if chunk == 0:
+            for load in loads[1:]:
+                load.wait()
         th, tl = th_ref[chunk], tl_ref[chunk]
         res = lax.dot_general(th, bh, dims, preferred_element_type=jnp.float32)
         res += lax.dot_general(th, bl, dims, preferred_element_type=jnp.float32)
@@ -132,12 +146,14 @@
             for g in range(groups):
                 sendbuf[pl.ds(((chunk * n_devices + e) * groups + g) * SUB, SUB), :] = (
                     res[e * SUB:(e + 1) * SUB, g * LANES:(g + 1) * LANES])
+        if chunk == 0:
+            pl.semaphore_wait(barrier, len(peers))
+        if chunk < RADIX - 1:
+            send(chunk)
         z += jnp.dot(cf_ref[chunk], res, precision=lax.Precision.HIGHEST, preferred_element_type=jnp.float32)
         sq = jnp.sum((res * res).reshape(-1, SUB, rows_count), 0)
         for g in range(groups):
             squares += sq[:, g * LANES:(g + 1) * LANES]
-        if chunk == 0:
-            pl.semaphore_wait(barrier, len(peers))
         if chunk == RADIX - 1:
             cosr, sinr, zr, zi = cr_ref[0:1, :], cr_ref[1:2, :], z[0:1, :], z[1:2, :]
             zre, zim = zr * cosr + zi * sinr, zi * cosr - zr * sinr
@@ -148,9 +164,32 @@
             stats[pl.ds(slot, 1)] = stat_out[...][None]
             for n in range(len(peers)):
                 stat_copy(n).start()
+            send(chunk)
+
+    def out_copy(g):
+        rows = pl.ds(g * 2 * LANES, 2 * LANES)
+        return pltpu.make_async_copy(out_ref.at[rows], out_hbm.at[rows], out_sem.at[g])
+
+    def finish_sums():
         for n in range(len(peers)):
-            data_copy(chunk, n).start()
-        own_copy(chunk).start()
+            stat_copy(n).wait_recv()
+        t0 = t1 = t2 = jnp.zeros((SUB, LANES), jnp.float32)
+        for q in range(n_devices):
+            angle = 2.0 * math.pi * q / total_len
+            v = stats[q]
+            t0, t1, t2 = t0 + v, t1 + v * math.cos(angle), t2 + v * math.sin(angle)
+        re = t1[1:2] + t2[2:3]
+        im = t1[2:3] - t2[1:2]
+        sums = jnp.concatenate([t0[0:1], re, im, jnp.zeros((SUB - 3, LANES), jnp.float32)], 0)
+        sums = jnp.sum(sums, 1, keepdims=True)
+        mean_square = jnp.broadcast_to(sums[0:1], (SUB, LANES)) / total_len
+        shifted = mean_square + 1e-06
+        factor = lax.rsqrt(shifted)
+        factor = factor * (1.5 - 0.5 * shifted * factor * factor)
+        scaled = factor / math.sqrt(total_len)
+        lane = lax.broadcasted_iota(jnp.int32, (SUB, LANES), 1)
+        fac_ref[...] = factor
+        tot_ref[...] = jnp.where(lane == 0, mean_square, jnp.where(lane == 1, sums[1:2], sums[2:3]) * scaled)
 
     gbits = groups.bit_length() - 1
     for chunk in range(RADIX):
@@ -165,22 +204,22 @@
             turned = swap_sublanes(tile.T.reshape(LANES // SUB, SUB, LANES))
             for a in range(LANES // SUB):
                 out_ref[pl.ds((g * LANES + rev(a, 4)) * 2 + h % 2, SUB, stride=2 * LANES // SUB), :] = turned[a]
-
-    for n in range(len(peers)):
-        stat_copy(n).wait_recv()
-    t0 = t1 = t2 = jnp.zeros((SUB, LANES), jnp.float32)
-    for q in range(n_devices):
-        angle = 2.0 * math.pi * q / total_len
-        v = stats[q]
-        t0, t1, t2 = t0 + v, t1 + v * math.cos(angle), t2 + v * math.sin(angle)
-    re = t1[1:2] + t2[2:3]
-    im = t1[2:3] - t2[1:2]
-    sums = jnp.concatenate([t0[0:1], re, im, jnp.zeros((SUB - 3, LANES), jnp.float32)], 0)
-    tot_ref[...] = jnp.broadcast_to(jnp.sum(sums, 1, keepdims=True), (SUB, LANES))
+            if h % 2:
+                out_copy(g).start()
+        if chunk == RADIX - 2:
+            finish_sums()
+    for g in range(RADIX * SUB // 2):
+        out_copy(g).wait()
     for n in range(len(peers)):
         stat_copy(n).wait_send()
         for chunk in range(RADIX):
             data_copy(chunk, n).wait_send()
+
+
+def scale_kernel(field_ref, tot_ref, fac_ref, out_ref, checks_ref):
+    field = field_ref[...]
+    out_ref[...] = (field.reshape(-1, SUB, LANES) * fac_ref[...][None]).reshape(field.shape)
+    checks_ref[...] = tot_ref[0:1, 0:3]
 
 
 def fast(n_outer, n_inner, amplitudes):
@@ -194,12 +233,18 @@
     tl = (table - th.astype(np.float32)).astype(jnp.bfloat16)
     vmem = pl.BlockSpec(memory_space=pltpu.VMEM)
     n_peers = n_devices - 1
-    field, tot = pl.pallas_call(
+    field, tot, fac = pl.pallas_call(
         functools.partial(kernel, n_outer, n_inner, rows_count, total_len),
-        out_shape=(jax.ShapeDtypeStruct(view.shape, jnp.float32), jax.ShapeDtypeStruct((SUB, LANES), jnp.float32)),
-        in_specs=[vmem] * 5,
-        out_specs=(vmem, vmem),
+        out_shape=(jax.ShapeDtypeStruct(view.shape, jnp.float32), *[jax.ShapeDtypeStruct((SUB, LANES), jnp.float32)] * 2),
+        in_specs=[pl.BlockSpec(memory_space=pltpu.HBM)] * 5,
+        out_specs=(pl.BlockSpec(memory_space=pltpu.HBM), vmem, vmem),
         scratch_shapes=[
+            pltpu.VMEM(view.shape, jnp.float32),
+            pltpu.VMEM(th.shape, jnp.bfloat16),
+            pltpu.VMEM(tl.shape, jnp.bfloat16),
+            pltpu.VMEM(cf.shape, jnp.float32),
+            pltpu.VMEM(cr.shape, jnp.float32),
+            pltpu.VMEM(view.shape, jnp.float32),
             pltpu.VMEM(view.shape, jnp.float32),
             pltpu.VMEM(view.shape, jnp.float32),
             pltpu.VMEM((SUB, LANES), jnp.float32),
@@ -209,16 +254,25 @@
             pltpu.SemaphoreType.DMA((RADIX,)),
             pltpu.SemaphoreType.DMA((n_peers,)),
             pltpu.SemaphoreType.DMA((n_peers,)),
+            pltpu.SemaphoreType.DMA((5,)),
+            pltpu.SemaphoreType.DMA((RADIX * SUB // 2,)),
         ],
         compiler_params=pltpu.CompilerParams(collective_id=0, has_side_effects=True,
-                                             vmem_limit_bytes=32 * 2**20),
+                                             vmem_limit_bytes=63_500_000),
     )(view, jnp.asarray(th), jnp.asarray(tl), jnp.asarray(cf), jnp.asarray(cr))
-    mean_square = tot[0, 0] / total_len
-    factor = lax.rsqrt(mean_square + 1e-06)
-    scaled = factor / math.sqrt(total_len)
-    checks = jnp.stack([mean_square, tot[1, 0] * scaled, tot[2, 0] * scaled])
-    result = (field * factor).reshape(-1, 2, LANES).transpose(1, 0, 2).reshape(2, amp_dev)
-    return result, checks
+    steps = 4
+    rows = pl.BlockSpec((view.shape[0] // steps, LANES), lambda k: (k, 0))
+    small = pl.BlockSpec((SUB, LANES), lambda k: (0, 0))
+    field, checks = pl.pallas_call(
+        scale_kernel,
+        grid=(steps,),
+        out_shape=(jax.ShapeDtypeStruct(view.shape, jnp.float32), jax.ShapeDtypeStruct((1, 3), jnp.float32)),
+        in_specs=[rows, small, small],
+        out_specs=(rows, pl.BlockSpec((1, 3), lambda k: (0, 0))),
+        compiler_params=pltpu.CompilerParams(vmem_limit_bytes=63_500_000),
+    )(field, tot, fac)
+    result = field.reshape(-1, 2, LANES).transpose(1, 0, 2).reshape(2, amp_dev)
+    return result, checks.reshape(3)
 
 
 def reverse_index(values, count):

time: 70.8 us -> 65.2 us (0.921)
  local copies, waits for them, and re-layouts: 5.66 us -> 0 us
  Pallas kernels: 60.1 us -> 64.3 us
  other arithmetic: 2.04 us -> 0 us
  between operations: 2.55 us -> 0.64 us
    unnamed x10 -> x0, local copies, waits for them, and re-layouts: 5.14 us -> none
    pallas_call x0 -> x1, Pallas kernels: none -> 3.8 us  [fast(): pl.pallas_call(scale_kernel, grid=(steps,), out_shape=(jax.ShapeDtypeStru...]
    mul x1 -> x0, other arithmetic: 1.45 us -> none  [fast(): field * factor]
where the time goes in v1:
time: 65.2 us; the launch traced here: 65 us
  Pallas kernels  64.3 us (99%)
    pallas_call x1, Pallas kernels, fast(): pl.pallas_call(functools.partial(kernel, n_outer, n_inner, rows_count, to...  60.5 us
    pallas_call x1, Pallas kernels, fast(): pl.pallas_call(scale_kernel, grid=(steps,), out_shape=(jax.ShapeDtypeStru...  3.8 us

profile of v1, /device:TPU:0, one launch (start us, length us, event | category | flops | bytes accessed | tf_op | source)
XLA Modules:
  0.0 65.0 jit_solution(5686213486920742878)
XLA Ops:
  0.6 60.5 %shard_map.68 = (f32[4096,128]{1,0:T(8,128)}, f32[8,128]{1,0:T(8,128)}, f32[8,128]{1,0:T(8,128)}) custom-call(f32[4096,128]{1,0:T(8,128)} %bitcast.11, bf16[4,256,256]{2,1,0:T(8,128)(2,1)} %constant.8.clone.th_hbm, bf16[4,256,256]{2,1,0:T(8,128)(2,1)} %constant.9.clone.tl_hbm, f32[4,8,256]{2,1,0:T(8,128)} %constant.10.clone.cf_hbm, ...), custom_call_target="tpu_custom_call" | custom-call | tf_op jit(solution)/shard_map/pallas_call | solution.py:236
  61.2 3.8 %shard_map.69 = (f32[4096,128]{1,0:T(8,128)}, f32[1,3]{1,0:T(1,128)}) custom-call(f32[4096,128]{1,0:T(8,128)} %get-tuple-element.7.field_ref, f32[8,128]{1,0:T(8,128)} %get-tuple-element.8.tot_ref, f32[8,128]{1,0:T(8,128)} %get-tuple-element.9.fac_ref), custom_call_target="tpu_custom_call" | custom-call | tf_op jit(solution)/shard_map/pallas_call | solution.py:266

commit v2 on v1

--- a/solution.py
+++ b/solution.py
@@ -10,6 +10,7 @@
 from jax.sharding import PartitionSpec as P
 
 WINDOW = 9
+STEPS = 8
 COLUMNS = 2**WINDOW
 LANES = 128
 SUB = 8
@@ -216,10 +217,20 @@
             data_copy(chunk, n).wait_send()
 
 
-def scale_kernel(field_ref, tot_ref, fac_ref, out_ref, checks_ref):
-    field = field_ref[...]
-    out_ref[...] = (field.reshape(-1, SUB, LANES) * fac_ref[...][None]).reshape(field.shape)
+def scale_kernel(field_hbm, tot_ref, fac_ref, out_hbm, checks_ref, field, out, sem):
+    size = field.shape[0] // STEPS
+    pieces = [pl.ds(k * size, size) for k in range(STEPS)]
+    loads = [pltpu.make_async_copy(field_hbm.at[p], field.at[p], sem.at[0, k]) for k, p in enumerate(pieces)]
+    stores = [pltpu.make_async_copy(out.at[p], out_hbm.at[p], sem.at[1, k]) for k, p in enumerate(pieces)]
+    for load in loads:
+        load.start()
     checks_ref[...] = tot_ref[0:1, 0:3]
+    for piece, load, store in zip(pieces, loads, stores):
+        load.wait()
+        out[piece, :] = (field[piece, :].reshape(-1, SUB, LANES) * fac_ref[...][None]).reshape(size, LANES)
+        store.start()
+    for store in stores:
+        store.wait()
 
 
 def fast(n_outer, n_inner, amplitudes):
@@ -260,15 +271,17 @@
         compiler_params=pltpu.CompilerParams(collective_id=0, has_side_effects=True,
                                              vmem_limit_bytes=63_500_000),
     )(view, jnp.asarray(th), jnp.asarray(tl), jnp.asarray(cf), jnp.asarray(cr))
-    steps = 4
-    rows = pl.BlockSpec((view.shape[0] // steps, LANES), lambda k: (k, 0))
-    small = pl.BlockSpec((SUB, LANES), lambda k: (0, 0))
+    hbm = pl.BlockSpec(memory_space=pltpu.HBM)
     field, checks = pl.pallas_call(
         scale_kernel,
-        grid=(steps,),
         out_shape=(jax.ShapeDtypeStruct(view.shape, jnp.float32), jax.ShapeDtypeStruct((1, 3), jnp.float32)),
-        in_specs=[rows, small, small],
-        out_specs=(rows, pl.BlockSpec((1, 3), lambda k: (0, 0))),
+        in_specs=[hbm, vmem, vmem],
+        out_specs=(hbm, vmem),
+        scratch_shapes=[
+            pltpu.VMEM(view.shape, jnp.float32),
+            pltpu.VMEM(view.shape, jnp.float32),
+            pltpu.SemaphoreType.DMA((2, STEPS)),
+        ],
         compiler_params=pltpu.CompilerParams(vmem_limit_bytes=63_500_000),
     )(field, tot, fac)
     result = field.reshape(-1, 2, LANES).transpose(1, 0, 2).reshape(2, amp_dev)

time: 65.2 us -> 65 us (level)
  no operation moved by 1% of the time
where the time goes in v2:
time: 65 us; the launch traced here: 64.8 us
  Pallas kernels  64.2 us (99%)
    pallas_call x1, Pallas kernels, fast(): pl.pallas_call(functools.partial(kernel, n_outer, n_inner, rows_count, to...  60.5 us
    pallas_call x1, Pallas kernels, fast(): pl.pallas_call(scale_kernel, out_shape=(jax.ShapeDtypeStruct(view.shape,...  3.61 us

profile of v2, /device:TPU:0, one launch (start us, length us, event | category | flops | bytes accessed | tf_op | source)
XLA Modules:
  0.0 64.8 jit_solution(3339069071101458703)
XLA Ops:
  0.6 60.5 %shard_map.68 = (f32[4096,128]{1,0:T(8,128)}, f32[8,128]{1,0:T(8,128)}, f32[8,128]{1,0:T(8,128)}) custom-call(f32[4096,128]{1,0:T(8,128)} %bitcast.11, bf16[4,256,256]{2,1,0:T(8,128)(2,1)} %constant.8.clone.th_hbm, bf16[4,256,256]{2,1,0:T(8,128)(2,1)} %constant.9.clone.tl_hbm, f32[4,8,256]{2,1,0:T(8,128)} %constant.10.clone.cf_hbm, ...), custom_call_target="tpu_custom_call" | custom-call | tf_op jit(solution)/shard_map/pallas_call | solution.py:247
  61.2 3.6 %shard_map.69 = (f32[4096,128]{1,0:T(8,128)}, f32[1,3]{1,0:T(1,128)}) custom-call(f32[4096,128]{1,0:T(8,128)} %get-tuple-element.7.field_hbm, f32[8,128]{1,0:T(8,128)} %get-tuple-element.8.tot_ref, f32[8,128]{1,0:T(8,128)} %get-tuple-element.9.fac_ref), custom_call_target="tpu_custom_call" | custom-call | tf_op jit(solution)/shard_map/pallas_call | solution.py:275
